TPU v7x, 512 devices: a 8x2x16 block of a 8x16x16 slice. The times are simulated.
512 devices in a mesh: groups: 2 (over y), seq: 32 (over z, core), rep: 8 (over x).
Axes of the slice: x: 8, y: 2, z: 16, core: 2. Of those that a mesh axis runs over, the one named last changes fastest.
The devices are a block of a 8x16x16 slice.
Arguments:
- queries: bfloat16 [1024, 4096], P(('groups', 'seq'), 'rep'), parts along dimension 0, may hold values from -128 to 128
- keys_new: bfloat16 [1024, 1024], P(('groups', 'seq'), 'rep'), parts along dimension 0, may hold values from -4 to 4
- values_new: bfloat16 [1024, 1024], P(('groups', 'seq'), 'rep'), parts along dimension 0, may hold values from -6 to 6
- keys_past: bfloat16 [16384, 1024], P(('groups', 'seq'), 'rep'), parts along dimension 0, may hold values from -4 to 4
- values_past: bfloat16 [16384, 1024], P(('groups', 'seq'), 'rep'), parts along dimension 0, may hold values from -6 to 6
- block_order: int32 [64], P('groups'), parts along dimension 0, may hold values from 0 to 31, each once
- residual: bfloat16 [1024, 4096], P(('groups', 'seq'), 'rep'), parts along dimension 0, may hold values from -6 to 6
- out_proj: bfloat16 [4096, 4096], P('seq', 'rep'), may hold values from -0.09375 to 0.09375
- norm_gain: float32 [4096], replicated, may hold values from 0.5 to 1.5
- router: float32 [4096, 4], replicated, may hold values from -0.09375 to 0.09375
- w_gate: bfloat16 [8, 4096, 4096], P('rep', None, 'seq'), may hold values from -0.09375 to 0.09375
- w_up: bfloat16 [8, 4096, 4096], P('rep', None, 'seq'), may hold values from -0.09375 to 0.09375
- w_down: bfloat16 [8, 4096, 4096], P('rep', 'seq'), may hold values from -0.0625 to 0.0625
- expert_ids: int32 [1024, 2], P(('groups', 'seq')), parts along dimension 0, may hold values from 0 to 3, all different within a row; in each aligned block of 16 rows (0 to 15, 16 to 31, ...) at most 12 rows name the same one
Outputs:
- attended: bfloat16 [1024, 4096], P(('groups', 'seq'), 'rep'), parts along dimension 0
- layer_out: bfloat16 [1024, 4096], P(('groups', 'seq'), 'rep'), parts along dimension 0
- keys_cache: bfloat16 [1024, 1024], P(('groups', 'seq')), parts along dimension 0
- values_cache: bfloat16 [1024, 1024], P(('groups', 'seq')), parts along dimension 0
There are 2 independent parts, one for each index of `groups`. A program takes and returns all parts, laid end to end along the dimension named above; an argument that names none is the same for every part. Nothing has to cross between parts.
Inputs may be any that keep to these rules, and one draw needn't show every extreme that they name: `block_order`: each block index 0 to 32 - 1 appears once. `expert_ids`: each row names 2 different experts; in the rows of one device (aligned blocks of 16 rows) no expert is named by more than 12 rows, and in some block one expert is named by exactly 12.
All inputs are finite; a program needn't handle non-finite values.
Results may differ from a plain program's by a relative error of at most 0.011.
Values may be sent and summed in bfloat16 or wider, within the bound.
A program may use at most 64 MiB of HBM per device.

v0:
```python
import math

import jax
import jax.numpy as jnp
from jax import lax
from jax.sharding import Mesh
from jax.sharding import PartitionSpec as P

EXPERTS = 4
CAP = 12
SEQ = ("seq_0", "seq_1")
GROUPS_SEQ = ("groups", "seq_0", "seq_1")


def in_one_piece(arrays, axis, dim, along):
    both = jnp.concatenate(arrays, axis=along)
    out, at, gathered = (lax.all_gather(both, axis, axis=dim, tiled=True), 0, [])
    for a in arrays:
        gathered.append(lax.slice_in_dim(out, at, at + a.shape[along], axis=along))
        at += a.shape[along]
    return tuple(gathered)


def sent_to_all(array, axis):
    size = lax.axis_size(axis)
    return lax.all_to_all(
        jnp.broadcast_to(array[None], (size, *array.shape)), axis, 0, 0, tiled=True
    )


def laid_out(tiles, dim):
    tiles = jnp.moveaxis(tiles, 0, dim)
    shape = tiles.shape
    return tiles.reshape(*shape[:dim], shape[dim] * shape[dim + 1], *shape[dim + 2 :])


def gather_directly(array, axis, dim):
    tiles = sent_to_all(array, axis)
    return laid_out(tiles, dim)


def own_block(tiles, axes, order):
    shape = [lax.axis_size(a) for a in axes]
    tiles = tiles.reshape(*shape, *tiles.shape[1:])
    tiles = tiles.transpose(*order, *range(len(axes), tiles.ndim))
    tiles = tiles.reshape(-1, *tiles.shape[len(axes) :])
    for k in order:
        tiles = lax.psum_scatter(tiles, axes[k], scatter_dimension=0, tiled=True)
    return tiles[0]


def in_blocks(array, dim, size):
    shape = array.shape
    tiles = array.reshape(*shape[:dim], size, shape[dim] // size, *shape[dim + 1 :])
    return jnp.moveaxis(tiles, dim, 0)


def sum_by_axis(array, axes, order, dim):
    size = lax.axis_size(axes)
    return own_block(in_blocks(array, dim, size), axes, order)


def block_lookup(owners, block_order):
    width = block_order.shape[0]
    hits = owners[:, None] == jnp.arange(width, dtype=jnp.int32)[None, :]
    return jnp.sum(jnp.where(hits, block_order[None, :], 0), axis=1)


def body(
    queries,
    keys_new,
    values_new,
    keys_past,
    values_past,
    block_order,
    residual,
    out_proj,
    norm_gain,
    router,
    w_gate,
    w_up,
    w_down,
    expert_ids,
):
    seq_index = lax.axis_index(SEQ)
    rep_index = lax.axis_index("rep")
    rep_count = lax.axis_size("rep")
    tok_count = queries.shape[0]
    head_dim = keys_new.shape[1]
    q_per = queries.shape[1] // head_dim
    past_len = keys_past.shape[0]
    key_span = past_len + tok_count
    row_total = tok_count * q_per
    my_block = block_lookup(jnp.full((1,), seq_index, jnp.int32), block_order)[0]
    scaling = 1.0 / math.sqrt(head_dim)
    query_rows = queries.reshape(row_total, head_dim)
    query_pos = my_block * tok_count + jnp.arange(row_total, dtype=jnp.int32) // q_per
    keys_local = jnp.concatenate([keys_past, keys_new], axis=0)
    values_local = jnp.concatenate([values_past, values_new], axis=0)
    running = jnp.full((row_total,), -1e30, jnp.float32)
    key_piece, value_piece = in_one_piece((keys_local, values_local), SEQ, 0, 1)
    row_count = key_piece.shape[0]
    key_index = jnp.arange(row_count, dtype=jnp.int32)
    key_owner = key_index // key_span
    offset = key_index % key_span
    key_pos = block_lookup(key_owner, block_order) * tok_count + offset - past_len
    visible = (offset < past_len)[None, :] | (key_pos[None, :] <= query_pos[:, None])
    scores = jnp.dot(query_rows, key_piece.T, preferred_element_type=jnp.float32) * scaling
    highest = jnp.maximum(running, jnp.max(jnp.where(visible, scores, -1e30), axis=1))
    weights = jnp.where(visible, jnp.exp(scores - highest[:, None]), 0.0)
    totals = jnp.sum(weights, axis=1)
    numerator = jnp.dot(
        weights.astype(jnp.bfloat16), value_piece, preferred_element_type=jnp.float32
    )
    running, totals, numerator = (highest, totals, numerator)
    attn_local = (
        (numerator / totals[:, None]).reshape(tok_count, q_per * head_dim).astype(jnp.bfloat16)
    )
    attn_full, keys_cache, values_cache = (
        lax.all_gather(attn_local, "rep", axis=1, tiled=True),
        *in_one_piece((keys_new, values_new), "rep", 1, 0),
    )
    projected = jnp.dot(
        attn_full,
        lax.all_gather(out_proj, SEQ, axis=0, tiled=True),
        preferred_element_type=jnp.float32,
    )
    attended = (residual.astype(jnp.float32) + projected).astype(jnp.bfloat16)
    full_rows = gather_directly(attended, "rep", 1)
    features = full_rows.astype(jnp.float32)
    mean_square = jnp.mean(features * features, axis=1, keepdims=True)
    normed = (features * norm_gain[None, :] * lax.rsqrt(mean_square + 1e-05)).astype(jnp.bfloat16)
    logits = jnp.dot(normed.astype(jnp.float32), router, precision=lax.Precision.HIGHEST)
    expert_range = jnp.arange(EXPERTS, dtype=jnp.int32)
    first_pick = (expert_ids[:, 0:1] == expert_range[None, :]).astype(jnp.float32)
    second_pick = (expert_ids[:, 1:2] == expert_range[None, :]).astype(jnp.float32)
    share_first = jax.nn.sigmoid(
        jnp.sum(first_pick * logits, axis=1) - jnp.sum(second_pick * logits, axis=1)
    )
    token_share = share_first[:, None] * first_pick + (1.0 - share_first)[:, None] * second_pick
    member = first_pick + second_pick
    ranking = jnp.cumsum(member, axis=0) - member
    slot_range = jnp.arange(CAP, dtype=jnp.float32)
    selection = member.T[:, None, :] * (ranking.T[:, None, :] == slot_range[None, :, None]).astype(
        jnp.float32
    )
    mine_mask = (expert_range == rep_index % EXPERTS).astype(jnp.float32)
    my_selection = jnp.einsum("e,ejt->jt", mine_mask, selection)
    slot_rows = jnp.dot(
        my_selection.astype(jnp.bfloat16), normed, preferred_element_type=jnp.float32
    ).astype(jnp.bfloat16)
    gate_local = w_gate[0]
    up_local = w_up[0]
    down_local = w_down[0]
    piece = lax.all_gather(slot_rows, SEQ, axis=0, tiled=True)
    gate_part = jnp.dot(piece, gate_local, preferred_element_type=jnp.float32)
    up_part = jnp.dot(piece, up_local, preferred_element_type=jnp.float32)
    hidden_slots = (jax.nn.silu(gate_part) * up_part).astype(jnp.bfloat16)
    expert_part = sum_by_axis(
        jnp.dot(hidden_slots, down_local, preferred_element_type=jnp.float32).astype(jnp.bfloat16),
        SEQ,
        (1, 0),
        0,
    ).astype(jnp.float32)
    returned = lax.all_to_all(
        expert_part.astype(jnp.bfloat16), "rep", split_axis=1, concat_axis=0, tiled=True
    ).astype(expert_part.dtype)
    source_expert = jnp.arange(rep_count, dtype=jnp.int32) % EXPERTS
    source_pick = (source_expert[:, None] == expert_range[None, :]).astype(jnp.float32)
    combine = jnp.einsum("re,ejt,te->trj", source_pick, selection, token_share).reshape(
        tok_count, rep_count * CAP
    )
    moe_slice = jnp.dot(combine, returned, precision=lax.Precision.HIGHEST)
    layer_out = (attended.astype(jnp.float32) + moe_slice).astype(jnp.bfloat16)
    return (attended, layer_out, keys_cache, values_cache)


def solution(mesh):
    split = Mesh(
        mesh.devices.reshape(mesh.shape["groups"], 16, 2, mesh.shape["rep"]),
        ("groups", "seq_0", "seq_1", "rep"),
    )
    return jax.shard_map(
        body,
        mesh=split,
        in_specs=(
            P(GROUPS_SEQ, "rep"),
            P(GROUPS_SEQ, "rep"),
            P(GROUPS_SEQ, "rep"),
            P(GROUPS_SEQ, "rep"),
            P(GROUPS_SEQ, "rep"),
            P("groups"),
            P(GROUPS_SEQ, "rep"),
            P(SEQ, "rep"),
            P(),
            P(),
            P("rep", None, SEQ),
            P("rep", None, SEQ),
            P("rep", SEQ, None),
            P(GROUPS_SEQ, None),
        ),
        out_specs=(
            P(GROUPS_SEQ, "rep"),
            P(GROUPS_SEQ, "rep"),
            P(GROUPS_SEQ, None),
            P(GROUPS_SEQ, None),
        ),
        check_vma=False,
    )
```

profile of v0, /device:TPU:80, one launch (start us, length us, event | category | flops | bytes accessed | tf_op | source)
XLA Modules:
  0.0 434.9 jit_solution(9324647808169427397)
XLA Ops:
  7.2 0.0 copy-start
  7.2 0.1 all-gather.5.cloned.1.call-start
  7.3 1.7 maximum_maximum_fusion
  8.9 0.1 all-gather.5.cloned.1.call-update
  9.0 0.1 all-gather.7.cloned.1.call-start
  9.0 0.7 all-gather.7.cloned.1.call-update
  9.8 0.7 reshape.156
  10.5 1.3 fusion.64
  12.5 0.9 select_reduce_fusion.1
  13.5 105.3 %all-gather.5.cloned.1.call-done = bf16[8704,256]{1,0:T(8,128)(2,1)} async-done(((bf16[272,256]{1,0:T(8,128)(2,1)}), bf16[8704,256]{1,0:T(8,128)(2,1)}) %all-gather.5.cloned.1.call-update) | async-done | bytes 4456464 | tf_op jit(solution)/shard_map/all_gather | solution.py:17
  118.9 2.8 select_reduce_fusion
  121.7 0.9 fusion.5
  122.5 0.8 fusion.22
  123.4 25.7 %all_gather.16 = bf16[16,4096]{1,0:T(8,128)(2,1)S(1)} all-gather(bf16[16,512]{1,0:T(8,128)(2,1)S(1)} %convert_element_type.81), channel_id=1, replica_groups=mesh['groups'=2,'seq_0'=16,'seq_1'=2,'rep'=8] {'rep'}, dimensions={1}, use_global_device_ids=true | all-gather | bytes 147456 | tf_op jit(solution)/shard_map/all_gather | solution.py:120
  149.1 43.8 %all-gather.7.cloned.1.call-done = bf16[4096,512]{1,0:T(8,128)(2,1)} async-done(((bf16[128,512]{1,0:T(8,128)(2,1)}), bf16[4096,512]{1,0:T(8,128)(2,1)}) %all-gather.7.cloned.1.call-update) | async-done | bytes 4194320 | tf_op jit(solution)/shard_map/all_gather | solution.py:125
  192.9 2.8 fusion.16
  195.7 0.7 broadcast_in_dim.33
  196.4 6.7 %all-to-all-start = ((bf16[8,16,512]{2,1,0:T(8,128)(2,1)}), bf16[8,16,512]{2,1,0:T(8,128)(2,1)S(1)}, u32[]{:S(2)}, u32[]{:S(2)}) async-start(bf16[8,16,512]{2,1,0:T(8,128)(2,1)} %broadcast_in_dim.33), calls=%async_computation | async-start | bytes 262144 | tf_op jit(solution)/shard_map/all_to_all | solution.py:26
  203.1 0.1 all-gather.9.cloned.1.call-start
  203.2 9.4 %all-to-all-done = bf16[8,16,512]{2,1,0:T(8,128)(2,1)S(1)} async-done(((bf16[8,16,512]{2,1,0:T(8,128)(2,1)}), bf16[8,16,512]{2,1,0:T(8,128)(2,1)S(1)}, u32[]{:S(2)}, u32[]{:S(2)}) %all-to-all-start) | async-done | bytes 131104 | tf_op jit(solution)/shard_map/all_to_all | solution.py:26
  212.6 0.1 fusion.32
  212.8 0.3 select_reduce_fusion.2
  213.2 0.1 copy.48
  213.3 0.1 copy.49
  213.4 0.1 fusion.47
  213.5 0.9 fusion.1
  214.4 0.1 all-gather.9.cloned.1.call-update
  214.5 0.1 reduce-scatter.3.cloned.1.call-start
  214.5 67.3 %all-gather.9.cloned.1.call-done = bf16[32,12,4096]{2,1,0:T(8,128)(2,1)} async-done(((bf16[1,12,4096]{2,1,0:T(8,128)(2,1)}), bf16[32,12,4096]{2,1,0:T(8,128)(2,1)}) %all-gather.9.cloned.1.call-update) | async-done | bytes 3145744 | tf_op jit(solution)/shard_map/all_gather | solution.py:155
  281.9 5.6 %reshape.160 = bf16[384,4096]{1,0:T(8,128)(2,1)} reshape(bf16[32,12,4096]{2,1,0:T(8,128)(2,1)} %all-gather.9.cloned.1.call-done) | data formatting | bytes 6291456
  287.5 2.9 fusion.30
  290.4 7.0 %convolution_convert_fusion = bf16[384,4096]{1,0:T(8,128)(2,1)} fusion(bf16[384,4096]{1,0:T(8,128)(2,1)} %reshape.160, bf16[1,128,4096]{2,1,0:T(8,128)(2,1)S(1)} %copy-done, bf16[1,4096,128]{2,1,0:T(8,128)(2,1)S(1)} %copy-done.2, f32[384,128]{1,0:T(8,128)S(1)} %fusion.30), kind=kOutput, calls=%fused_computation.2 | convolution fusion | flops 807174144 | bytes 8585216 | tf_op jit(solution)/shard_map/dot_general | solution.py:160
  297.5 5.5 %reshape_reshape.3 = bf16[16,2,12,4096]{3,2,1,0:T(8,128)(2,1)} reshape(bf16[384,4096]{1,0:T(8,128)(2,1)} %convolution_convert_fusion) | data formatting | bytes 6291456 | tf_op jit(solution)/shard_map/reshape;reshape | solution.py:44
  302.9 5.6 %copy.51 = bf16[2,16,12,4096]{3,1,0,2:T(8,128)(2,1)} copy(bf16[2,16,12,4096]{3,2,0,1:T(8,128)(2,1)} %bitcast.62) | data formatting | bytes 6291456 | tf_op jit(solution)/shard_map/transpose | solution.py:45
  308.5 0.1 reduce-scatter.3.cloned.1.call-update
  308.6 0.2 reduce-scatter.5.cloned.1.call-start
  308.9 19.5 %reduce-scatter.3.cloned.1.call-done = bf16[16,12,4096]{2,0,1:T(8,128)(2,1)} async-done(((bf16[32,12,4096]{2,0,1:T(8,128)(2,1)}), bf16[16,12,4096]{2,0,1:T(8,128)(2,1)}) %reduce-scatter.3.cloned.1.call-update) | async-done | bytes 1572880 | tf_op jit(solution)/shard_map/reduce_scatter | solution.py:48
  328.4 3.7 copy.52
  332.1 0.1 reduce-scatter.5.cloned.1.call-update
  332.2 23.7 %all_gather.19 = bf16[32,1024]{1,0:T(8,128)(2,1)S(1)} all-gather(bf16[32,128]{1,0:T(8,128)(2,1)S(1)} %pad_maximum_fusion), channel_id=1, replica_groups=mesh['groups'=2,'seq_0'=16,'seq_1'=2,'rep'=8] {'rep'}, dimensions={1}, use_global_device_ids=true | all-gather | bytes 73728 | tf_op jit(solution)/shard_map/all_gather | solution.py:17
  355.9 0.6 fusion.72
  356.5 53.6 %reduce-scatter.5.cloned.1.call-done = bf16[1,12,4096]{2,1,0:T(8,128)(2,1)} async-done(((bf16[16,12,4096]{2,1,0:T(8,128)(2,1)}), bf16[1,12,4096]{2,1,0:T(8,128)(2,1)}) %reduce-scatter.5.cloned.1.call-update) | async-done | bytes 98320 | tf_op jit(solution)/shard_map/reduce_scatter | solution.py:48
  410.1 0.9 copy.57
  411.1 0.7 copy.53
  411.8 6.6 %all-to-all-start.1 = ((bf16[12,8,512]{2,0,1:T(8,128)(2,1)}), bf16[12,8,512]{2,0,1:T(8,128)(2,1)S(1)}, u32[]{:S(2)}, u32[]{:S(2)}) async-start(bf16[12,8,512]{2,0,1:T(8,128)(2,1)} %copy.53), calls=%async_computation.3 | async-start | bytes 262144 | tf_op jit(solution)/shard_map/all_to_all | solution.py:165
  418.4 0.2 convolution_bitcast_fusion
  418.6 8.9 %all-to-all-done.1 = bf16[12,8,512]{2,0,1:T(8,128)(2,1)S(1)} async-done(((bf16[12,8,512]{2,0,1:T(8,128)(2,1)}), bf16[12,8,512]{2,0,1:T(8,128)(2,1)S(1)}, u32[]{:S(2)}, u32[]{:S(2)}) %all-to-all-start.1) | async-done | bytes 98336 | tf_op jit(solution)/shard_map/all_to_all | solution.py:165
  427.5 0.8 fusion.15
  (38 shorter events, 0.3 us)
Async XLA Ops:
  7.2 283.2 %copy-start = (bf16[1,128,4096]{2,1,0:T(8,128)(2,1)S(1)}, bf16[1,128,4096]{2,1,0:T(8,128)(2,1)}, u32[]{:S(2)}) copy-start(bf16[1,128,4096]{2,1,0:T(8,128)(2,1)} %param.26) | copy-start | bytes 3145732
  7.2 111.7 %all-gather.5.cloned.1.call-start = ((), (), s32[]{:S(2)}) async-start(), calls=%async_computation.4 | async-start | bytes 4595712 | tf_op jit(solution)/shard_map/all_gather | solution.py:17
  9.0 183.9 %all-gather.7.cloned.1.call-start = ((), (), s32[]{:S(2)}) async-start(), calls=%async_computation.5 | async-start | bytes 4325376 | tf_op jit(solution)/shard_map/all_gather | solution.py:125
  118.9 3.7 copy-start.10
  122.5 70.4 %copy-start.6 = (bf16[16,512]{1,0:T(8,128)(2,1)S(1)}, bf16[16,512]{1,0:T(8,128)(2,1)}, u32[]{:S(2)}) copy-start(bf16[16,512]{1,0:T(8,128)(2,1)} %param.20) | copy-start | bytes 49156
  149.1 54.1 %copy-start.9 = (s32[16,2]{0,1:T(2,128)S(1)}, s32[16,2]{0,1:T(2,128)}, u32[]{:S(2)}) copy-start(s32[16,2]{0,1:T(2,128)} %param.27) | copy-start | bytes 388
  149.1 63.7 %copy-start.4 = (f32[4096,4]{0,1:T(4,128)S(1)}, f32[4096,4]{0,1:T(4,128)}, u32[]{:S(2)}) copy-start(f32[4096,4]{0,1:T(4,128)} %param.23) | copy-start | bytes 196612
  149.1 63.7 %copy-start.5 = (f32[4096]{0:T(1024)S(1)}, f32[4096]{0:T(1024)}, u32[]{:S(2)}) copy-start(f32[4096]{0:T(1024)} %param.22) | copy-start | bytes 49156
  195.7 231.8 %copy-start.3 = (bf16[16,512]{1,0:T(8,128)(2,1)}, bf16[16,512]{1,0:T(8,128)(2,1)S(1)}, u32[]{:S(2)}) copy-start(bf16[16,512]{1,0:T(8,128)(2,1)S(1)} %fusion.16) | copy-start | bytes 49156
  196.4 16.2 %all-to-all-start = ((bf16[8,16,512]{2,1,0:T(8,128)(2,1)}), bf16[8,16,512]{2,1,0:T(8,128)(2,1)S(1)}, u32[]{:S(2)}, u32[]{:S(2)}) async-start(bf16[8,16,512]{2,1,0:T(8,128)(2,1)} %broadcast_in_dim.33), calls=%async_computation | async-start | bytes 262144 | tf_op jit(solution)/shard_map/all_to_all | solution.py:26
  203.1 78.7 %all-gather.9.cloned.1.call-start = ((), (), s32[]{:S(2)}) async-start(), calls=%async_computation.8 | async-start | bytes 4325376 | tf_op jit(solution)/shard_map/all_gather | solution.py:155
  214.5 73.0 %copy-start.1 = (bf16[1,4096,128]{2,1,0:T(8,128)(2,1)S(1)}, bf16[1,4096,128]{2,1,0:T(8,128)(2,1)}, u32[]{:S(2)}) copy-start(bf16[1,4096,128]{2,1,0:T(8,128)(2,1)} %param.24) | copy-start | bytes 3145732
  214.5 113.9 %reduce-scatter.3.cloned.1.call-start = ((), (), s32[]{:S(2)}) async-start(), calls=%async_computation.6 | async-start | bytes 4718592 | tf_op jit(solution)/shard_map/reduce_scatter | solution.py:48
  287.5 3.0 copy-start.2
  308.6 23.5 %copy-start.7 = (bf16[16,128]{1,0:T(8,128)(2,1)S(1)}, bf16[16,128]{1,0:T(8,128)(2,1)}, u32[]{:S(2)}) copy-start(bf16[16,128]{1,0:T(8,128)(2,1)} %param.16) | copy-start | bytes 12292
  308.6 23.5 %copy-start.8 = (bf16[16,128]{1,0:T(8,128)(2,1)S(1)}, bf16[16,128]{1,0:T(8,128)(2,1)}, u32[]{:S(2)}) copy-start(bf16[16,128]{1,0:T(8,128)(2,1)} %param.15) | copy-start | bytes 12292
  308.6 101.5 %reduce-scatter.5.cloned.1.call-start = ((), (), s32[]{:S(2)}) async-start(), calls=%async_computation.7 | async-start | bytes 2228224 | tf_op jit(solution)/shard_map/reduce_scatter | solution.py:48
  411.8 15.7 %all-to-all-start.1 = ((bf16[12,8,512]{2,0,1:T(8,128)(2,1)}), bf16[12,8,512]{2,0,1:T(8,128)(2,1)S(1)}, u32[]{:S(2)}, u32[]{:S(2)}) async-start(bf16[12,8,512]{2,0,1:T(8,128)(2,1)} %copy.53), calls=%async_computation.3 | async-start | bytes 262144 | tf_op jit(solution)/shard_map/all_to_all | solution.py:165
Sparse Core Ops, SparseCore 0:
  10.2 108.6 all-gather.4
  121.0 71.8 all-gather.6
  214.6 67.2 all-gather.8
  308.7 19.6 reduce-scatter.2
  332.2 77.8 reduce-scatter.4
where the time goes:
time: 436 us; the launch traced here: 435 us
  waiting for transfers between devices  309 us (71%)
  blocking collectives  49.4 us (11%)
  local copies, waits for them, and re-layouts  24.3 us (6%)
  matrix products  18.8 us (4%)
  between operations  14.7 us (3%)
  starting transfers between devices  13.8 us (3%)
  other arithmetic  5.04 us (1%)
    all_gather x1, waiting for transfers between devices, in_one_piece(): lax.all_gather(both, axis, axis=dim, tiled=True)  105 us
    reduce_scatter x2, waiting for transfers between devices, own_block(): tiles = lax.psum_scatter(tiles, axes[k], scatter_dimension=0, tiled=True)  73.1 us
    all_gather x1, waiting for transfers between devices, body(): piece = lax.all_gather(slot_rows, SEQ, axis=0, tiled=True)  67.3 us
    all_gather x1, waiting for transfers between devices, body(): lax.all_gather(out_proj, SEQ, axis=0, tiled=True)  43.8 us
    all_gather x1, blocking collectives, body(): lax.all_gather(attn_local, 'rep', axis=1, tiled=True)  25.7 us
    all_gather x1, blocking collectives, in_one_piece(): lax.all_gather(both, axis, axis=dim, tiled=True)  23.7 us
    all_to_all x1, waiting for transfers between devices, sent_to_all(): lax.all_to_all(jnp.broadcast_to(array[None], (size, *array.shape)), axis,...  9.35 us
    all_to_all x1, waiting for transfers between devices, body(): lax.all_to_all(expert_part.astype(jnp.bfloat16), 'rep', split_axis=1, con...  8.89 us
  transfers between devices with their start and end apart: 7, of which 7 were waited for; matrix products, arithmetic and copies ran while one was open for 2% of the time, Pallas kernels for 0%

commit v1 on v0

v1 whole, which is shorter than its diff:
```python
import functools
import math

import jax
import jax.numpy as jnp
from jax import lax
from jax.experimental import pallas as pl
from jax.experimental.pallas import tpu as pltpu
from jax.sharding import PartitionSpec as P

MESH = pl.DeviceIdType.MESH
BF16 = jnp.bfloat16
F32 = jnp.float32
EXPERTS = 4
CAP = 12
CORES = 2
STRIDES = 4


def iota(shape, dim):
    return lax.broadcasted_iota(jnp.int32, shape, dim)


def remote(src, dst, send, recv, device):
    return pltpu.make_async_remote_copy(
        src_ref=src,
        dst_ref=dst,
        send_sem=send,
        recv_sem=recv,
        device_id=device,
        device_id_type=MESH,
    )


def place():
    seq = lax.axis_index("seq")
    return seq // CORES, seq % CORES, lax.axis_index("rep")


def greet(devices):
    barrier = pltpu.get_barrier_semaphore()
    for device in devices:
        pl.semaphore_signal(barrier, inc=1, device_id=device, device_id_type=MESH)
    pl.semaphore_wait(barrier, len(devices))


def attention_kernel(
    nz,
    nr,
    order_ref,
    q_ref,
    kn_ref,
    vn_ref,
    kp_ref,
    vp_ref,
    res_ref,
    wo_ref,
    att_ref,
    full_ref,
    kc_ref,
    vc_ref,
    qbuf,
    qrows,
    kv,
    wall,
    osend,
    lsend,
    orecv,
    lrecv,
    oall,
    aall,
    kcs,
    vcs,
    loc,
    qs,
    qr,
    ks,
    kr,
    ds,
    dr,
    ws,
    wr,
    es,
    er,
    cs,
    cr,
    vs,
    vr,
    os_,
    or_,
    ls,
    lr,
    xs,
    xr,
    as_,
    ar,
):
    z, c, r = place()
    tok, width = q_ref.shape
    hd = kn_ref.shape[1]
    q_per = width // hd
    past = kp_ref.shape[0]
    half = past // 2
    block = past + tok
    first = tok + half
    stride = nz // STRIDES
    reach = stride // 2
    rows = tok * q_per
    window = kv.shape[1]
    depth = wo_ref.shape[0]
    scale = 1.0 / math.sqrt(hd)

    def at_z(offset, core=None):
        return lax.rem(z + (offset % nz), nz) * CORES + (c if core is None else core)

    def seq(offset, core=None):
        return {"seq": at_z(offset, core)}

    other = {"seq": z * CORES + (1 - c)}
    columns = [lax.rem(r + j, nr) for j in range(nr)]
    across = [{"rep": columns[j]} for j in range(nr)]

    def base(offset):
        return half + (offset + reach - 1) * block

    def kv_at(core, start, size):
        return kv.at[core, pl.ds(start, size), :]

    own = base(0)
    local = [
        pltpu.make_async_copy(q_ref, qbuf.at[0], loc.at[0]),
        pltpu.make_async_copy(kn_ref, kv.at[0, pl.ds(own, tok), pl.ds(0, hd)], loc.at[1]),
        pltpu.make_async_copy(vn_ref, kv.at[0, pl.ds(own, tok), pl.ds(hd, hd)], loc.at[2]),
        pltpu.make_async_copy(kp_ref, kv.at[0, pl.ds(own + tok, past), pl.ds(0, hd)], loc.at[3]),
        pltpu.make_async_copy(vp_ref, kv.at[0, pl.ds(own + tok, past), pl.ds(hd, hd)], loc.at[4]),
    ]

    def w_rows(offset, part=None):
        start = at_z(offset) * depth
        size = depth
        if part is not None:
            size = depth // 2
            start = start + part * size
        return wall.at[pl.ds(pl.multiple_of(start, depth // 2), size), :]

    w_local = pltpu.make_async_copy(wo_ref, w_rows(0), loc.at[5])
    for copy in local:
        copy.start()
    w_local.start()

    greet(
        [seq(1), seq(-1), other]
        + [seq(stride * j) for j in range(1, STRIDES)]
        + [across[j] for j in range(1, nr)]
    )
    pending = []

    def go(copy):
        copy.start()
        pending.append(copy)
        return copy

    local[0].wait()
    q_copies = {}
    for j in (2, 1, 3):
        slot = (STRIDES - j) % STRIDES
        q_copies[slot] = go(
            remote(qbuf.at[0], qbuf.at[slot], qs.at[slot], qr.at[slot], seq(stride * j))
        )
    for copy in local[1:]:
        copy.wait()
    k_right = {1: go(remote(kv_at(0, own, block), kv_at(0, base(-1), block), ks.at[0], kr.at[0], seq(1)))}
    k_left = {1: go(remote(kv_at(0, own, block), kv_at(0, base(1), block), ks.at[1], kr.at[1], seq(-1)))}

    dies = []

    def to_other(start, size):
        n = len(dies)
        dies.append(go(remote(kv_at(0, start, size), kv_at(1, start, size), ds.at[n], dr.at[n], other)))

    to_other(own, block)

    w_local.wait()

    def w_send(t):
        if t < nz // 2:
            return [
                (go(remote(w_rows(1 - t), w_rows(1 - t), ws.at[t], wr.at[t], seq(1))), -t, None),
                (go(remote(w_rows(t - 1), w_rows(t - 1), ws.at[nz - t], wr.at[nz - t], seq(-1))), t, None),
            ]
        return [
            (go(remote(w_rows(1 - t, 0), w_rows(1 - t, 0), ws.at[t], wr.at[t], seq(1))), -t, 0),
            (go(remote(w_rows(t - 1, 1), w_rows(t - 1, 1), ws.at[0], wr.at[0], seq(-1))), t, 1),
        ]

    w_dies = []

    def w_other(offset, part=None):
        n = len(w_dies)
        view = w_rows(offset, part)
        w_dies.append(go(remote(view, view, es.at[n], er.at[n], other)))

    flight = w_send(1)
    w_other(0)
    k_copies = []
    v_copies = []
    mine = pl.ds(pl.multiple_of(r * hd, hd), hd)
    for j in range(1, nr):
        k_copies.append(
            go(remote(kv.at[0, pl.ds(own, tok), pl.ds(0, hd)], kcs.at[:, mine], cs.at[j], cr.at[j], across[j]))
        )
        v_copies.append(
            go(remote(kv.at[0, pl.ds(own, tok), pl.ds(hd, hd)], vcs.at[:, mine], vs.at[j], vr.at[j], across[j]))
        )
    kcs[:, mine] = kv[0, own : own + tok, 0:hd]
    vcs[:, mine] = kv[0, own : own + tok, hd : 2 * hd]

    k_right[1].wait_recv()
    k_right[2] = go(
        remote(kv_at(0, base(-1) + first, half), kv_at(0, 0, half), ks.at[2], kr.at[2], seq(1))
    )
    to_other(base(-1), block)
    k_left[1].wait_recv()
    k_left[2] = go(
        remote(kv_at(0, base(1), first), kv_at(0, base(2), first), ks.at[3], kr.at[3], seq(-1))
    )
    to_other(base(1), block)

    step = [1]

    def w_step():
        nonlocal flight
        arrived = flight
        step[0] += 1
        if step[0] > nz // 2 + 1:
            return
        for copy, offset, part in arrived:
            copy.wait_recv()
        if step[0] <= nz // 2:
            flight = w_send(step[0])
        else:
            flight = []
        for copy, offset, part in arrived:
            w_other(offset, part)

    w_step()
    k_right[2].wait_recv()
    to_other(0, half)
    k_left[2].wait_recv()
    to_other(base(2), first)
    lane = iota((1, CORES * window), 1)
    kpos = jnp.full((1, CORES * window), -1, jnp.int32)
    for cc in range(CORES):
        core = c if cc == 0 else 1 - c
        for offset in range(1 - reach, reach + 1):
            rel = lane - (cc * window + base(offset))
            spot = order_ref[at_z(offset, core)] * tok + rel
            kpos = jnp.where((rel >= 0) & (rel < tok), spot, kpos)
    row = iota((rows, 1), 0)
    eye = iota((rows, hd), 0) == iota((rows, hd), 1)

    def partial(slot):
        for h in range(q_per):
            qrows[h * tok : (h + 1) * tok, :] = qbuf[slot, :, h * hd : (h + 1) * hd]
        qpos = order_ref[at_z(stride * slot)] * tok + lax.rem(row, tok)
        keys = kv[:, :, 0:hd].reshape(CORES * window, hd)
        values = kv[:, :, hd : 2 * hd].reshape(CORES * window, hd)
        s = lax.dot_general(
            qrows[...], keys, (((1,), (1,)), ((), ())), preferred_element_type=F32
        )
        s = jnp.where(kpos <= qpos, s * scale, -1e30)
        top = jnp.max(s, axis=1, keepdims=True)
        p = jnp.exp(s - top)
        total = jnp.sum(p, axis=1, keepdims=True)
        o = jnp.dot(p.astype(BF16), values, preferred_element_type=F32)
        return o / total, top + jnp.log(total)

    q_copies[1].wait_recv()
    q_copies[3].wait_recv()
    for copy in dies:
        copy.wait_recv()
    o_copies = {}
    for slot in (1, 3, 2):
        if slot == 2:
            q_copies[2].wait_recv()
        o, lse = partial(slot)
        osend[slot] = o.astype(BF16)
        lsend[slot] = jnp.broadcast_to(
            jnp.sum(jnp.where(eye, lse, 0.0), axis=0, keepdims=True), lsend.shape[1:]
        )
        to = (STRIDES - slot) % STRIDES
        o_copies[to] = (
            go(remote(osend.at[slot], orecv.at[to], os_.at[to], or_.at[to], seq(stride * slot))),
            go(remote(lsend.at[slot], lrecv.at[to], ls.at[to], lr.at[to], seq(stride * slot))),
        )
        w_step()
    o, lse = partial(0)
    w_step()
    outs, logs = [o], [lse]
    for slot in (1, 3, 2):
        for copy in o_copies[slot]:
            copy.wait_recv()
        outs.append(orecv[slot].astype(F32))
        logs.append(jnp.sum(jnp.where(eye, lrecv[slot][0:1, :], 0.0), axis=1, keepdims=True))
    top = functools.reduce(jnp.maximum, logs)
    shares = [jnp.exp(x - top) for x in logs]
    total = functools.reduce(jnp.add, shares)
    heads = functools.reduce(jnp.add, [a * b for a, b in zip(outs, shares)]) / total
    heads = heads.astype(BF16)
    for h in range(q_per):
        oall[r, :, h * hd : (h + 1) * hd] = heads[h * tok : (h + 1) * tok, :]
    x_copies = [
        go(remote(oall.at[r], oall.at[r], xs.at[j], xr.at[j], across[j])) for j in range(1, nr)
    ]
    while step[0] <= nz // 2:
        w_step()
    for copy in x_copies:
        copy.wait_recv()
    for copy in w_dies:
        copy.wait_recv()
    projected = jnp.zeros((tok, width), F32)
    for j in range(nr):
        projected = projected + jnp.dot(
            oall[j], wall[j * width : (j + 1) * width, :], preferred_element_type=F32
        )
    attended = (res_ref[...].astype(F32) + projected).astype(BF16)
    aall[r] = attended
    a_copies = [
        go(remote(aall.at[r], aall.at[r], as_.at[j], ar.at[j], across[j])) for j in range(1, nr)
    ]
    att_ref[...] = attended
    for copy in k_copies + v_copies:
        copy.wait_recv()
    kc_ref[...] = kcs[...]
    vc_ref[...] = vcs[...]
    for copy in a_copies:
        copy.wait_recv()
    full_ref[...] = aall[...]
    for copy in pending:
        copy.wait_send()


def experts_kernel(
    nz,
    nr,
    idv_ref,
    ids_ref,
    x_ref,
    gain_ref,
    router_ref,
    wg_ref,
    wu_ref,
    wd_ref,
    out_ref,
    wgu,
    wd,
    ring,
    rows_all,
    stacked,
    parts,
    right_in,
    left_in,
    mine,
    back,
    loc,
    ds,
    dr,
    gs,
    gr,
    rs,
    rr,
    xs,
    xr,
):
    z, c, r = place()
    _, tok, width = x_ref.shape
    hidden = wg_ref.shape[2]
    packed = nr * CAP
    padded = nr * tok
    n_parts = 2
    piece = packed // n_parts
    expert = lax.rem(r, EXPERTS)

    def seq(offset):
        return {"seq": lax.rem(z + (offset % nz), nz) * CORES + c}

    other = {"seq": z * CORES + (1 - c)}
    across = [{"rep": lax.rem(r + j, nr)} for j in range(nr)]
    up_at = CORES * hidden
    loads = [
        pltpu.make_async_copy(wg_ref.at[0], wgu.at[:, pl.ds(0, hidden)], loc.at[0]),
        pltpu.make_async_copy(wu_ref.at[0], wgu.at[:, pl.ds(up_at, hidden)], loc.at[1]),
        pltpu.make_async_copy(wd_ref.at[0], wd.at[pl.ds(0, hidden), :], loc.at[2]),
    ]
    for copy in loads:
        copy.start()
    greet([seq(1), seq(-1), other] + across[1:])
    pending = []

    def go(copy):
        copy.start()
        pending.append(copy)
        return copy

    x = x_ref[...].astype(F32)
    square = jnp.sum(jnp.sum(x * x, axis=0), axis=1, keepdims=True) / (nr * width)
    normed = (x * gain_ref[...].reshape(nr, 1, width) * lax.rsqrt(square + 1e-05)[None]).astype(BF16)

    lane = iota((1, padded), 1)
    line = iota((padded, 1), 0)
    lane_rank = jnp.full((1, padded), -padded, jnp.int32)
    line_rank = jnp.full((padded, 1), -padded, jnp.int32)
    count = jnp.int32(0)
    for t in range(tok):
        member = (ids_ref[t, 0] == expert) | (ids_ref[t, 1] == expert)
        rank = jnp.where(member, count, -padded)
        count = count + jnp.where(member, 1, 0)
        lane_rank = jnp.where(lax.rem(lane, tok) == t, rank, lane_rank)
        line_rank = jnp.where(lax.rem(line, tok) == t, rank, line_rank)

    def one_hot(mask):
        return jnp.where(mask, 1.0, 0.0).astype(BF16)

    choose = one_hot(iota((packed, padded), 0) == (lane // tok) * CAP + lane_rank)
    put_back = one_hot(iota((padded, packed), 1) == (line // tok) * CAP + line_rank)
    spot = lax.rem(line, tok)
    widen = one_hot(
        iota((padded, packed), 1) == jnp.where(spot < CAP, (line // tok) * CAP + spot, -1)
    )
    spot = lax.rem(lane, tok)
    narrow = one_hot(
        iota((packed, padded), 0) == jnp.where(spot < CAP, (lane // tok) * CAP + spot, -1)
    )

    ring[0] = jnp.dot(
        choose, normed.reshape(padded, width), preferred_element_type=F32
    ).astype(BF16)

    def part(ref, slot, p):
        return ref.at[slot, pl.ds(p * piece, piece), :]

    mid = nz // 2
    right, left = {}, {}

    def gather_send(t):
        for p in range(n_parts):
            if t < mid or p == 0:
                right[t, p] = go(
                    remote(part(ring, t - 1, p), part(ring, t, p), gs.at[0, t, p], gr.at[0, t, p], seq(1))
                )
            if t < mid or p == 1:
                left[t, p] = go(
                    remote(
                        part(ring, (nz - t + 1) % nz, p),
                        part(ring, nz - t, p),
                        gs.at[1, t, p],
                        gr.at[1, t, p],
                        seq(-1),
                    )
                )

    gather_send(1)
    swaps = [
        go(remote(wg_ref.at[0], wgu.at[:, pl.ds(hidden, hidden)], ds.at[0], dr.at[0], other)),
        go(remote(wu_ref.at[0], wgu.at[:, pl.ds(up_at + hidden, hidden)], ds.at[1], dr.at[1], other)),
        go(remote(wd_ref.at[0], wd.at[pl.ds(hidden, hidden), :], ds.at[2], dr.at[2], other)),
    ]

    logits = []
    for e in range(EXPERTS):
        column = router_ref[e * nr : (e + 1) * nr, :].reshape(nr, 1, width)
        logits.append(jnp.sum(jnp.sum(normed.astype(F32) * column, axis=0), axis=1, keepdims=True))
    one, two = idv_ref[:, 0:1], idv_ref[:, 1:2]
    first = functools.reduce(jnp.add, [jnp.where(one == e, logits[e], 0.0) for e in range(EXPERTS)])
    second = functools.reduce(jnp.add, [jnp.where(two == e, logits[e], 0.0) for e in range(EXPERTS)])
    share = jax.nn.sigmoid(first - second)
    shares = [
        jnp.where(one == e, share, 0.0) + jnp.where(two == e, 1.0 - share, 0.0)
        for e in range(EXPERTS)
    ]

    arrival = [0]
    for t in range(1, mid):
        arrival += [t, nz - t]
    arrival.append(mid)
    group = nz // 2

    def lay_out(i):
        wide = jnp.dot(widen, ring[arrival[i]], preferred_element_type=F32).astype(BF16)
        for f in range(nr):
            rows_all[i * tok : (i + 1) * tok, f * width : (f + 1) * width] = wide[
                f * tok : (f + 1) * tok, :
            ]

    def compute(start, count):
        sel = slice(start * tok, (start + count) * tok)
        gate = jnp.dot(rows_all[sel, :], wgu[:, 0:up_at], preferred_element_type=F32)
        up = jnp.dot(rows_all[sel, :], wgu[:, up_at : 2 * up_at], preferred_element_type=F32)
        act = (gate * jax.nn.sigmoid(gate) * up).astype(BF16)
        for f in range(nr):
            y = jnp.dot(
                act, wd[:, f * width : (f + 1) * width], preferred_element_type=F32
            ).astype(BF16)
            for i in range(count):
                stacked[start + i, f * tok : (f + 1) * tok, :] = y[i * tok : (i + 1) * tok, :]
        for i in range(start, start + count):
            parts[arrival[i]] = jnp.dot(
                narrow, stacked[i], preferred_element_type=F32
            ).astype(BF16)

    lay_out(0)
    for t in range(1, mid + 1):
        for p in range(n_parts):
            if (t, p) in right:
                right[t, p].wait_recv()
            if (t, p) in left:
                left[t, p].wait_recv()
        if t < mid:
            gather_send(t + 1)
            lay_out(2 * t - 1)
            lay_out(2 * t)
        if t == mid // 2:
            for copy in loads:
                copy.wait()
            for copy in swaps:
                copy.wait_recv()
            compute(0, group)
    lay_out(nz - 1)
    compute(group, nz - group)

    sums = {}

    def reduce_send(way, t, p, src):
        into = right_in if way == 0 else left_in
        sums[way, t, p] = go(
            remote(src, part(into, t, p), rs.at[way, t, p], rr.at[way, t, p], seq(1 if way == 0 else -1))
        )

    def behind(way, t):
        return (nz - t) % nz if way == 0 else t % nz

    def begins(way, p):
        return mid if p == way else mid - 1

    for t in range(mid, 0, -1):
        for p in range(n_parts):
            for way in (0, 1):
                if t > begins(way, p):
                    continue
                slot = behind(way, t)
                if t == begins(way, p):
                    reduce_send(way, t, p, part(parts, slot, p))
                    continue
                into = right_in if way == 0 else left_in
                sums[way, t + 1, p].wait_recv()
                sel = slice(p * piece, (p + 1) * piece)
                into[t + 1, sel, :] = (
                    into[t + 1, sel, :].astype(F32) + parts[slot, sel, :].astype(F32)
                ).astype(BF16)
                reduce_send(way, t, p, part(into, t + 1, p))
    for p in range(n_parts):
        for way in (0, 1):
            sums[way, 1, p].wait_recv()
    total = (
        parts[0].astype(F32) + right_in[1].astype(F32) + left_in[1].astype(F32)
    ).astype(BF16)
    mine[...] = (
        jnp.dot(put_back, total, preferred_element_type=F32).astype(BF16).reshape(nr, tok, width)
    )
    x_copies = [
        go(remote(mine.at[lax.rem(r + j, nr)], back.at[r], xs.at[j], xr.at[j], across[j]))
        for j in range(1, nr)
    ]
    back[r] = mine[r]
    for copy in x_copies:
        copy.wait_recv()
    out = x_ref[r].astype(F32)
    for j in range(nr):
        out = out + shares[j % EXPERTS] * back[j].astype(F32)
    out_ref[...] = out.astype(BF16)
    for copy in pending:
        copy.wait_send()


def body(
    nz,
    nr,
    queries,
    keys_new,
    values_new,
    keys_past,
    values_past,
    block_order,
    residual,
    out_proj,
    norm_gain,
    router,
    w_gate,
    w_up,
    w_down,
    expert_ids,
):
    tok, width = queries.shape
    hd = keys_new.shape[1]
    past = keys_past.shape[0]
    q_per = width // hd
    rows = tok * q_per
    depth = out_proj.shape[0]
    hidden = w_gate.shape[2]
    model = nr * width
    window = (nz // STRIDES) * (past + tok)
    dma = pltpu.SemaphoreType.DMA
    vmem = pl.BlockSpec(memory_space=pltpu.VMEM)
    smem = pl.BlockSpec(memory_space=pltpu.SMEM)
    hbm = pl.BlockSpec(memory_space=pl.ANY)

    attended, full, keys_cache, values_cache = pl.pallas_call(
        functools.partial(attention_kernel, nz, nr),
        out_shape=(
            jax.ShapeDtypeStruct((tok, width), BF16),
            jax.ShapeDtypeStruct((nr, tok, width), BF16),
            jax.ShapeDtypeStruct((tok, nr * hd), BF16),
            jax.ShapeDtypeStruct((tok, nr * hd), BF16),
        ),
        in_specs=[smem, hbm, hbm, hbm, hbm, hbm, vmem, hbm],
        out_specs=(vmem, vmem, vmem, vmem),
        scratch_shapes=[
            pltpu.VMEM((STRIDES, tok, width), BF16),
            pltpu.VMEM((rows, hd), BF16),
            pltpu.VMEM((CORES, window, 2 * hd), BF16),
            pltpu.VMEM((CORES * nz * depth, width), BF16),
            pltpu.VMEM((STRIDES, rows, hd), BF16),
            pltpu.VMEM((STRIDES, 8, hd), F32),
            pltpu.VMEM((STRIDES, rows, hd), BF16),
            pltpu.VMEM((STRIDES, 8, hd), F32),
            pltpu.VMEM((nr, tok, width), BF16),
            pltpu.VMEM((nr, tok, width), BF16),
            pltpu.VMEM((tok, nr * hd), BF16),
            pltpu.VMEM((tok, nr * hd), BF16),
            dma((6,)),
            dma((STRIDES,)),
            dma((STRIDES,)),
            dma((4,)),
            dma((4,)),
            dma((5,)),
            dma((5,)),
            dma((nz,)),
            dma((nz,)),
            dma((nz + 1,)),
            dma((nz + 1,)),
            dma((nr,)),
            dma((nr,)),
            dma((nr,)),
            dma((nr,)),
            dma((STRIDES,)),
            dma((STRIDES,)),
            dma((STRIDES,)),
            dma((STRIDES,)),
            dma((nr,)),
            dma((nr,)),
            dma((nr,)),
            dma((nr,)),
        ],
        compiler_params=pltpu.CompilerParams(collective_id=0, has_side_effects=True),
        name="attention",
    )(
        block_order,
        queries,
        keys_new,
        values_new,
        keys_past,
        values_past,
        residual,
        out_proj,
    )
    packed = nr * CAP
    padded = nr * tok
    layer_out = pl.pallas_call(
        functools.partial(experts_kernel, nz, nr),
        out_shape=jax.ShapeDtypeStruct((tok, width), BF16),
        in_specs=[vmem, smem, vmem, vmem, vmem, hbm, hbm, hbm],
        out_specs=vmem,
        scratch_shapes=[
            pltpu.VMEM((model, 2 * CORES * hidden), BF16),
            pltpu.VMEM((CORES * hidden, model), BF16),
            pltpu.VMEM((nz, packed, width), BF16),
            pltpu.VMEM((nz * tok, model), BF16),
            pltpu.VMEM((nz, padded, width), BF16),
            pltpu.VMEM((nz, packed, width), BF16),
            pltpu.VMEM((nz // 2 + 1, packed, width), BF16),
            pltpu.VMEM((nz // 2 + 1, packed, width), BF16),
            pltpu.VMEM((nr, tok, width), BF16),
            pltpu.VMEM((nr, tok, width), BF16),
            dma((3,)),
            dma((3,)),
            dma((3,)),
            dma((2, nz // 2 + 1, 2)),
            dma((2, nz // 2 + 1, 2)),
            dma((2, nz // 2 + 1, 2)),
            dma((2, nz // 2 + 1, 2)),
            dma((nr,)),
            dma((nr,)),
        ],
        compiler_params=pltpu.CompilerParams(collective_id=1, has_side_effects=True),
        name="experts",
    )(
        expert_ids,
        expert_ids,
        full,
        norm_gain.reshape(nr, width),
        router.T.reshape(EXPERTS * nr, width),
        w_gate,
        w_up,
        w_down,
    )
    return attended, layer_out, keys_cache, values_cache


def solution(mesh):
    nz = mesh.shape["seq"] // CORES
    nr = mesh.shape["rep"]
    rows = P(("groups", "seq"), "rep")
    whole = P(("groups", "seq"), None)
    return jax.shard_map(
        functools.partial(body, nz, nr),
        mesh=mesh,
        in_specs=(
            rows,
            rows,
            rows,
            rows,
            rows,
            P("groups"),
            rows,
            P("seq", "rep"),
            P(),
            P(),
            P("rep", None, "seq"),
            P("rep", None, "seq"),
            P("rep", "seq", None),
            whole,
        ),
        out_specs=(rows, rows, whole, whole),
        check_vma=False,
    )
```

time: 436 us -> 192 us (0.44)
  waiting for transfers between devices: 309 us -> 0 us
  Pallas kernels: 0 us -> 184 us
  blocking collectives: 49.4 us -> 0 us
  matrix products: 18.8 us -> 0 us
  local copies, waits for them, and re-layouts: 24.3 us -> 6.88 us
  between operations: 14.7 us -> 0.69 us
  starting transfers between devices: 13.8 us -> 0 us
  other arithmetic: 5.04 us -> 0 us
    all_gather x3 -> x0, waiting for transfers between devices: 216 us -> none  [the longest x1 105 us: in_one_piece(): lax.all_gather(both, axis, axis=dim, tiled=True)]
    pallas_call x0 -> x2, Pallas kernels: none -> 184 us  [the longest x1 100 us: body(): pl.pallas_call(functools.partial(attention_kernel, nz, nr), out_shape=(ja...]
    reduce_scatter x2 -> x0, waiting for transfers between devices: 73.1 us -> none  [own_block(): tiles = lax.psum_scatter(tiles, axes[k], scatter_dimension=0, tiled=True)]
    all_gather x2 -> x0, blocking collectives: 49.4 us -> none  [the longest x1 25.7 us: body(): lax.all_gather(attn_local, 'rep', axis=1, tiled=True)]
    dot_general x10 -> x0, matrix products: 18.8 us -> none  [the longest x1 7.02 us: body(): jnp.dot(hidden_slots, down_local, preferred_element_type=jnp.float32)]
    all_to_all x2 -> x0, waiting for transfers between devices: 18.2 us -> none  [the longest x1 9.35 us: sent_to_all(): lax.all_to_all(jnp.broadcast_to(array[None], (size, *array.shape)), axis,...]
    all_to_all x2 -> x0, starting transfers between devices: 13.4 us -> none  [the longest x1 6.7 us: sent_to_all(): lax.all_to_all(jnp.broadcast_to(array[None], (size, *array.shape)), axis,...]
    transpose x1 -> x0, local copies, waits for them, and re-layouts: 5.59 us -> none  [own_block(): tiles = tiles.transpose(*order, *range(len(axes), tiles.ndim))]
  transfers between devices with their start and end apart: 7 -> 0, of which waited for: 7 -> 0; matrix products, arithmetic and copies ran while one was open for 2% -> 0% of each run, Pallas kernels for 0% -> 0%
where the time goes in v1:
time: 192 us
  Pallas kernels  184 us (96%)
  local copies, waits for them, and re-layouts  6.88 us (4%)
    pallas_call x1, Pallas kernels, body(): pl.pallas_call(functools.partial(attention_kernel, nz, nr), out_shape=(ja...  100 us
    pallas_call x1, Pallas kernels, body(): pl.pallas_call(functools.partial(experts_kernel, nz, nr), out_shape=jax.S...  84 us
    unnamed x15, local copies, waits for them, and re-layouts  4.05 us

profile of v1, /device:TPU:80, one launch (start us, length us, event | category | flops | bytes accessed | tf_op | source)
XLA Modules:
  0.0 191.7 jit_solution(1855219544590274922)
XLA Ops:
  0.6 0.0 copy-start.4
  0.6 0.7 copy-done.4
  1.3 0.7 copy.18.idv_ref.ids_ref
  2.0 1.3 reshape.14.gain_ref
  3.3 1.5 reshape.15.router_ref
  4.8 100.2 %attention.1 = (bf16[16,512]{1,0:T(8,128)(2,1)}, bf16[8,16,512]{2,1,0:T(8,128)(2,1)}, bf16[16,1024]{1,0:T(8,128)(2,1)}, bf16[16,1024]{1,0:T(8,128)(2,1)}) custom-call(s32[32]{0:T(128)} %order_ref.1, bf16[16,512]{1,0:T(8,128)(2,1)} %q_ref.1, bf16[16,128]{1,0:T(8,128)(2,1)} %kn_ref.1, bf16[16,128]{1,0:T(8,128)(2,1)} %vn_ref.1, bf16[256,128]{1,0:T(8,128)(2,1)} %kp_ref.1, ...), custom_call_target="tpu_custom_call" | custom-call | tf_op jit(solution)/shard_map/attention/pallas_call | solution.py:617
  105.0 0.0 copy-start.3
  105.0 84.0 %experts.1 = bf16[16,512]{1,0:T(8,128)(2,1)} custom-call(s32[16,2]{1,0:T(8,128)} %copy.18.idv_ref.ids_ref, s32[16,2]{1,0:T(8,128)} %copy.18.idv_ref.ids_ref, bf16[8,16,512]{2,1,0:T(8,128)(2,1)} %get-tuple-element.9.x_ref, f32[8,512]{1,0:T(8,128)} %reshape.14.gain_ref, f32[32,512]{1,0:T(8,128)} %reshape.15.router_ref, bf16[1,4096,128]{2,1,0:T(8,128)(2,1)} %wg_ref.1, ...), custom_call_target="tpu_custom_call" | custom-call | tf_op jit(solution)/shard_map/experts/pallas_call | solution.py:678
  189.0 0.0 copy-done.3
  189.0 0.0 copy-start
  189.0 0.0 copy-start.2
  189.0 0.6 copy.24
  189.7 0.1 copy-done
  189.7 0.6 copy.25
  190.3 0.0 copy-done.2
  190.3 0.0 copy-start.1
  190.4 0.6 copy.26
  191.0 0.2 copy-done.1
  191.1 0.6 copy.27
Async XLA Ops:
  0.6 0.7 copy-start.4
  105.0 84.0 %copy-start.3 = (bf16[16,512]{1,0:T(8,128)(2,1)S(1)}, bf16[16,512]{1,0:T(8,128)(2,1)}, u32[]{:S(2)}) copy-start(bf16[16,512]{1,0:T(8,128)(2,1)} %get-tuple-element.16) | copy-start | bytes 49156
  189.0 0.7 copy-start
  189.0 1.3 copy-start.2
  190.3 0.8 copy-start.1
